TPU v7x, 32 devices: a whole 2x2x4 slice. The times are simulated.
32 devices in a mesh: expert: 8 (over z, y), dp: 4 (over x, core).
Axes of the slice: x: 2, y: 2, z: 4, core: 2. Of those that a mesh axis runs over, the one named last changes fastest.
Arguments:
- tokens: bfloat16 [2048, 2880], P(('expert', 'dp')), may hold values from -6 to 6
- expert_ids: int32 [2048, 4], P(('expert', 'dp')), may hold values from 0 to 7, all different within a row; in each aligned block of 64 rows (0 to 63, 64 to 127, ...) at most 48 rows name the same one
- gate_logits: float32 [2048, 4], P(('expert', 'dp')), may hold values from -3 to 3
- w_gate: bfloat16 [8, 2880, 1536], P('expert', None, 'dp'), may hold values from -0.109375 to 0.109375
- w_up: bfloat16 [8, 2880, 1536], P('expert', None, 'dp'), may hold values from -0.109375 to 0.109375
- w_down: bfloat16 [8, 1536, 2880], P('expert', 'dp'), may hold values from -0.15625 to 0.15625
Outputs:
- mixed: bfloat16 [2048, 2880], P(('expert', 'dp'))
Inputs may be any that keep to these rules, and one draw needn't show every extreme that they name: `expert_ids`: each row names 4 different experts. Among the 64 rows of one device no expert is named more than 48 times, and every expert is named somewhere.
All inputs are finite; a program needn't handle non-finite values.
Results may differ from a plain program's by a relative error of at most 0.012.
Values may be sent and summed in bfloat16 or wider, within the bound.
A program may use at most 128 MiB of HBM per device.

v0:
```python
import functools

import jax
import jax.numpy as jnp
from jax import lax
from jax.experimental import pallas as pl
from jax.experimental.pallas import tpu as pltpu
from jax.sharding import PartitionSpec as P


def expert_rows(tile_in, gate_w, up_w, down_w):
    gate_val = jnp.dot(tile_in, gate_w, preferred_element_type=jnp.float32)
    up_val = jnp.dot(tile_in, up_w, preferred_element_type=jnp.float32)
    hidden = ((up_val + 1.0) * gate_val * jax.nn.sigmoid(1.702 * gate_val)).astype(jnp.bfloat16)
    return jnp.dot(hidden, down_w, preferred_element_type=jnp.float32).astype(jnp.bfloat16)


def run_tiles(packed, first_row, last_row, gate_w, up_w, down_w):
    tile_rows = 128
    n_tiles = jnp.maximum(last_row - first_row + tile_rows - 1, 0) // tile_rows
    result_buf = jnp.zeros((packed.shape[0], down_w.shape[1]), jnp.bfloat16)

    def advance(index_t, buffer):
        at_row = first_row + index_t * tile_rows
        tile_in = lax.dynamic_slice_in_dim(packed, at_row, tile_rows, 0)
        return lax.dynamic_update_slice_in_dim(
            buffer, expert_rows(tile_in, gate_w, up_w, down_w), at_row, 0
        )

    return lax.fori_loop(0, n_tiles, advance, result_buf)


def sparse_device(tokens, expert_ids, gate_logits, w_gate, w_up, w_down):
    n_rows, width = tokens.shape
    n_tops = expert_ids.shape[1]
    n_exp = lax.axis_size("expert")
    n_dp = lax.axis_size("dp")
    slot_cap = max(2, 3 * n_rows * n_tops // (2 * n_exp))
    tile_rows = 128
    flat_ids = expert_ids.reshape(-1)
    onehot = (flat_ids[:, None] == jnp.arange(n_exp, dtype=jnp.int32)[None, :]).astype(jnp.int32)
    rank_in = jnp.sum((jnp.cumsum(onehot, axis=0) - onehot) * onehot, axis=1)
    counts = jnp.sum(onehot, axis=0)
    slot_idx = flat_ids * slot_cap + rank_in
    source = (
        jnp.zeros((n_exp * slot_cap,), jnp.int32)
        .at[slot_idx]
        .set(jnp.arange(n_rows * n_tops, dtype=jnp.int32) // n_tops)
    )
    filled = (jnp.arange(slot_cap)[None, :] < counts[:, None]).reshape(-1)
    outgoing = jnp.where(filled[:, None], tokens[source], jnp.zeros_like(tokens[source])).reshape(
        n_exp, slot_cap, width
    )
    rows_mid, counts_mid = (
        lax.all_to_all(outgoing, "expert", split_axis=0, concat_axis=0, tiled=True),
        lax.all_to_all(counts[:, None], "expert", split_axis=0, concat_axis=0, tiled=True),
    )
    rows_in, counts_in = (
        lax.all_gather(rows_mid, "dp", axis=0, tiled=True),
        lax.all_gather(counts_mid, "dp", axis=0, tiled=True),
    )
    rows_flat = rows_in.reshape(-1, width)
    total_rows = rows_flat.shape[0]
    live_row = (jnp.arange(slot_cap)[None, :] < counts_in.reshape(-1)[:, None]).reshape(-1)
    position = jnp.cumsum(live_row.astype(jnp.int32)) - 1
    live_total = jnp.sum(live_row.astype(jnp.int32))
    padded = (total_rows + tile_rows - 1) // tile_rows * tile_rows + tile_rows
    gather_idx = (
        jnp.zeros((padded,), jnp.int32)
        .at[jnp.where(live_row, position, padded)]
        .set(jnp.arange(total_rows, dtype=jnp.int32), mode="drop")
    )
    packed = rows_flat[gather_idx]
    gate_w = w_gate[0]
    up_w = w_up[0]
    down_w = w_down[0]
    merged = run_tiles(packed, 0, live_total, gate_w, up_w, down_w)
    slot_out = jnp.where(
        live_row[:, None],
        merged[jnp.where(live_row, position, 0)],
        jnp.zeros((total_rows, width), jnp.bfloat16),
    )
    summed = lax.psum_scatter(
        slot_out.reshape(n_dp * n_exp, slot_cap, width), "dp", scatter_dimension=0, tiled=True
    ).astype(jnp.float32)
    expert_out = lax.all_to_all(
        summed.astype(jnp.bfloat16), "expert", split_axis=0, concat_axis=0, tiled=True
    )
    picked = expert_out.reshape(n_exp * slot_cap, width)[slot_idx]
    gate_wts = jnp.exp(gate_logits)
    gate_wts = gate_wts / jnp.sum(gate_wts, axis=1, keepdims=True)
    mixed = jnp.sum(
        picked.reshape(n_rows, n_tops, width).astype(jnp.float32) * gate_wts[:, :, None], axis=1
    )
    return mixed.astype(jnp.bfloat16)


LANES = 128
CHUNKS = 1


def round_up(value, step):
    return (value + step - 1) // step * step


def routing_columns(expert_ids, gate_logits, n_exp, lanes):
    gate_wts = jnp.exp(gate_logits)
    gate_wts = gate_wts / jnp.sum(gate_wts, axis=1, keepdims=True)
    chosen = expert_ids[:, :, None] == jnp.arange(n_exp, dtype=jnp.int32)[None, None, :]
    by_expert = jnp.sum(jnp.where(chosen, gate_wts[:, :, None], 0.0), axis=1)
    high = by_expert.astype(jnp.bfloat16)
    low = (by_expert - high.astype(jnp.float32)).astype(jnp.bfloat16)
    columns = jnp.concatenate([high, low], axis=1)
    return jnp.pad(columns, ((0, 0), (0, lanes - columns.shape[1])))


def dense_kernel(n_exp, rows_ref, gate_ref, up_ref, down_ref, out_ref):
    width, hidden_width = gate_ref.shape
    lanes = rows_ref.shape[1]
    mine = lax.axis_index("expert")
    rows_in = rows_ref[:, :width]
    gate_val = jnp.dot(rows_in, gate_ref[...], preferred_element_type=jnp.float32)
    up_val = jnp.dot(rows_in, up_ref[...], preferred_element_type=jnp.float32)
    first = width // LANES * LANES
    extra = rows_ref[:, first:lanes].astype(jnp.float32)
    lane = lax.broadcasted_iota(jnp.int32, extra.shape, 1) + first - width
    weight = jnp.sum(jnp.where((lane == mine) | (lane == mine + n_exp), extra, 0.0), axis=1, keepdims=True)
    hidden = (up_val + 1.0) * gate_val * (weight / (1.0 + jnp.exp(-1.702 * gate_val)))
    out_ref[...] = jnp.dot(
        hidden.astype(jnp.bfloat16), down_ref[...], preferred_element_type=jnp.float32
    ).astype(out_ref.dtype)


def dense_rows(rows, gate_w, up_w, down_w, n_exp):
    n_rows, lanes = rows.shape
    width, hidden_width = gate_w.shape
    tile_rows = 256
    while n_rows % tile_rows:
        tile_rows //= 2
    whole = pl.BlockSpec(memory_space=pltpu.VMEM)
    return pl.pallas_call(
        functools.partial(dense_kernel, n_exp),
        grid=(n_rows // tile_rows,),
        in_specs=[pl.BlockSpec((tile_rows, lanes), lambda i: (i, 0)), whole, whole, whole],
        out_specs=pl.BlockSpec((tile_rows, width), lambda i: (i, 0)),
        out_shape=jax.ShapeDtypeStruct((n_rows, width), jnp.bfloat16),
        cost_estimate=pl.CostEstimate(
            flops=6 * n_rows * width * hidden_width,
            bytes_accessed=2 * n_rows * (lanes + width) + 6 * width * hidden_width,
            transcendentals=n_rows * hidden_width,
        ),
    )(rows, gate_w, up_w, down_w)


def dense_device(tokens, expert_ids, gate_logits, w_gate, w_up, w_down):
    n_rows, width = tokens.shape
    n_exp = lax.axis_size("expert")
    both = ("expert", "dp")
    lanes = round_up(width + 2 * n_exp, LANES)
    extra = routing_columns(expert_ids, gate_logits, n_exp, lanes - width)
    wide = jnp.concatenate([tokens, extra], axis=1)
    step = n_rows // CHUNKS
    done = []
    for chunk in range(CHUNKS):
        rows = lax.all_gather(wide[chunk * step : (chunk + 1) * step], both, axis=0, tiled=True)
        partial = dense_rows(rows, w_gate[0], w_up[0], w_down[0], n_exp)
        done.append(lax.psum_scatter(partial, both, scatter_dimension=0, tiled=True))
    return done[0] if CHUNKS == 1 else jnp.concatenate(done, axis=0)


def tile_product(n_exp, rows_in, extra, gate_ref, up_ref, down_ref):
    width = gate_ref.shape[0]
    mine = lax.axis_index("expert")
    gate_val = jnp.dot(rows_in, gate_ref[...], preferred_element_type=jnp.float32)
    up_val = jnp.dot(rows_in, up_ref[...], preferred_element_type=jnp.float32)
    extra = extra.astype(jnp.float32)
    lane = lax.broadcasted_iota(jnp.int32, extra.shape, 1) - width % LANES
    weight = jnp.sum(jnp.where((lane == mine) | (lane == mine + n_exp), extra, 0.0), axis=1, keepdims=True)
    hidden = (up_val + 1.0) * gate_val * (weight / (1.0 + jnp.exp(-1.702 * gate_val)))
    return lax.dot_general(
        hidden.astype(jnp.bfloat16),
        down_ref[...],
        (((1,), (1,)), ((), ())),
        preferred_element_type=jnp.float32,
    )


def fused_kernel(
    n_exp, wide_ref, gate_hbm, up_hbm, down_hbm, out_ref,
    held, part, core_in, x_in, y_in, x_diag, y_diag, z_in,
    gate_ref, up_ref, down_ref, send_sem, recv_sem, load_sem,
):
    n_z = n_exp // 2
    n_rows, width = out_ref.shape
    lanes = wide_ref.shape[1]
    half = n_rows // 2
    spare = width // LANES * LANES
    expert, dp = lax.axis_index("expert"), lax.axis_index("dp")
    z, y = lax.div(expert, 2), lax.rem(expert, 2)
    x, core = lax.div(dp, 2), lax.rem(dp, 2)
    to_x = (expert, (1 - x) * 2 + core)
    to_y = (z * 2 + 1 - y, dp)
    to_core = (expert, x * 2 + 1 - core)

    def at_z(d):
        return lax.rem(z + d, n_z)

    def to_z(d):
        return (at_z(d) * 2 + y, dp)

    columns = {"o": y * 2 + x, "x": y * 2 + 1 - x, "y": (1 - y) * 2 + x, "d": (1 - y) * 2 + 1 - x}

    def block(column, which, zz=0):
        return (columns[column] * 2 + which) * n_z + zz

    copies = {}

    def start(key, source, target, device):
        number = len(copies)
        copies[key] = pltpu.make_async_remote_copy(
            src_ref=source,
            dst_ref=target,
            send_sem=send_sem.at[number],
            recv_sem=recv_sem.at[number],
            device_id=device,
            device_id_type=pl.DeviceIdType.MESH,
        )
        copies[key].start()

    def arrived(*key):
        copies[key].wait_recv()

    loads = [
        pltpu.make_async_copy(source, target, load_sem.at[i])
        for i, (source, target) in enumerate(((gate_hbm, gate_ref), (up_hbm, up_ref), (down_hbm, down_ref)))
    ]
    for load in loads:
        load.start()

    partners = [to_x, to_y, to_core] + [to_z(d) for d in range(1, n_z)]
    barrier = pltpu.get_barrier_semaphore()
    for partner in partners:
        pl.semaphore_signal(barrier, inc=1, device_id=partner, device_id_type=pl.DeviceIdType.MESH)
    pl.semaphore_wait(barrier, len(partners))

    near = sorted(range(1, n_z), key=lambda d: min(d, n_z - d))
    own = held.at[block("o", core, z)]
    start(("x", 0), wide_ref, own, to_x)
    start(("y", 0), wide_ref, own, to_y)
    for d in near:
        start(("z", d), wide_ref, own, to_z(d))
    start(("co", 0), wide_ref, own, to_core)
    own[...] = wide_ref[...]

    def relay_z(d):
        arrived("z", d)
        source = held.at[block("o", core, at_z(n_z - d))]
        start(("x", d), source, source, to_x)
        start(("y", d), source, source, to_y)
        start(("co", d), source, source, to_core)

    def relay_xy(d):
        zz = at_z(n_z - d)
        arrived("x", d)
        source = held.at[block("x", core, zz)]
        upper = held.at[block("x", core, zz), pl.ds(0, half)]
        start(("y2", d), upper, upper, to_y)
        start(("cx", d), source, source, to_core)
        arrived("y", d)
        source = held.at[block("y", core, zz)]
        lower = held.at[block("y", core, zz), pl.ds(half, half)]
        start(("x2", d), lower, lower, to_x)
        start(("cy", d), source, source, to_core)

    def relay_diag(d):
        source = held.at[block("d", core, at_z(n_z - d))]
        arrived("x2", d)
        arrived("y2", d)
        start(("cd", d), source, source, to_core)

    def product(column, which):
        span = pl.ds(block(column, which), n_z)
        rows_in = held[span, :, :width].reshape(n_z * n_rows, width)
        extra = held[span, :, spare:lanes].reshape(n_z * n_rows, lanes - spare)
        result = tile_product(n_exp, rows_in, extra, gate_ref, up_ref, down_ref)
        part[span] = result.astype(part.dtype).reshape(n_z, n_rows, width)

    order = "oxyd"

    def swap(column):
        for d in range(n_z):
            arrived("c" + column, d)
        product(column, 1 - core)
        start(("p", column), part.at[pl.ds(block(column, 1 - core), n_z)], core_in.at[order.index(column)], to_core)

    def combine(column):
        arrived("p", column)
        place = order.index(column)
        base = block(column, core)

        @pl.loop(0, n_z)
        def _(zz):
            part[base + zz] = part[base + zz] + core_in[place, zz]

    waiting = [0]
    for d in near:
        relay_z(d)
        if d == near[-1]:
            for load in loads:
                load.wait()
            product("o", core)
        relay_xy(waiting.pop())
        waiting.append(d)
    swap("o")
    relay_xy(waiting.pop())
    product("x", core)
    swap("x")
    relay_diag(0)
    product("y", core)
    for d in near[:-1]:
        relay_diag(d)
    combine("x")
    rows_x = pl.ds(block("x", core), n_z)
    start(("ex",), part.at[rows_x, pl.ds(half, half)], x_in.at[:, pl.ds(half, half)], to_x)
    swap("y")
    relay_diag(near[-1])
    product("d", core)
    combine("y")
    rows_y = pl.ds(block("y", core), n_z)
    start(("ey",), part.at[rows_y, pl.ds(0, half)], y_in.at[:, pl.ds(0, half)], to_y)
    swap("d")
    combine("d")
    far = near[::-1] + [0]
    for d in far:
        source = block("d", core, at_z(d))
        start(("dx", d), part.at[source, pl.ds(half, half)], x_diag.at[d], to_x)
        start(("dy", d), part.at[source, pl.ds(0, half)], y_diag.at[d], to_y)
    combine("o")

    def gather_diag(d):
        zz = at_z(d)
        arrived("dx", d)
        spot = block("y", core, zz)
        part[spot, half:] = part[spot, half:] + x_diag[d]
        start(("fy", d), part.at[spot, pl.ds(half, half)], y_in.at[zz, pl.ds(half, half)], to_y)
        arrived("dy", d)
        spot = block("x", core, zz)
        part[spot, :half] = part[spot, :half] + y_diag[d]
        start(("fx", d), part.at[spot, pl.ds(0, half)], x_in.at[zz, pl.ds(0, half)], to_x)

    def gather_xy(d):
        zz = at_z(d)
        arrived("fx", d)
        arrived("fy", d)
        total = (
            part[block("o", core, zz)].astype(jnp.float32)
            + x_in[zz].astype(jnp.float32)
            + y_in[zz].astype(jnp.float32)
        )
        if d == 0:
            for other in far[:-1]:
                arrived("s", other)
                total = total + z_in[other - 1].astype(jnp.float32)
            out_ref[...] = total.astype(out_ref.dtype)
        else:
            spot = block("o", core, zz)
            part[spot] = total.astype(part.dtype)
            start(("s", d), part.at[spot], z_in.at[d - 1], to_z(d))

    gather_diag(far[0])
    arrived("ex")
    arrived("ey")
    for before, d in zip(far, far[1:]):
        gather_diag(d)
        gather_xy(before)
    gather_xy(far[-1])
    for copy in copies.values():
        copy.wait_send()


def fused_device(tokens, expert_ids, gate_logits, w_gate, w_up, w_down):
    n_rows, width = tokens.shape
    hidden_width = w_gate.shape[2]
    n_exp = lax.axis_size("expert")
    n_z = n_exp // 2
    lanes = round_up(width + 2 * n_exp, LANES)
    extra = routing_columns(expert_ids, gate_logits, n_exp, lanes - width)
    wide = jnp.concatenate([tokens, extra], axis=1)
    total = n_exp * lax.axis_size("dp")
    messages = 8 * n_z + 4 * n_z + 4 + 2 + 4 * n_z + n_z + n_z
    bf16 = jnp.bfloat16
    in_vmem = pl.BlockSpec(memory_space=pltpu.VMEM)
    anywhere = pl.BlockSpec(memory_space=pl.ANY)
    return pl.pallas_call(
        functools.partial(fused_kernel, n_exp),
        in_specs=[in_vmem, anywhere, anywhere, anywhere],
        out_specs=in_vmem,
        out_shape=jax.ShapeDtypeStruct((n_rows, width), bf16),
        scratch_shapes=[
            pltpu.VMEM((total, n_rows, lanes), bf16),
            pltpu.VMEM((total, n_rows, width), bf16),
            pltpu.VMEM((4, n_z, n_rows, width), bf16),
            pltpu.VMEM((n_z, n_rows, width), bf16),
            pltpu.VMEM((n_z, n_rows, width), bf16),
            pltpu.VMEM((n_z, n_rows // 2, width), bf16),
            pltpu.VMEM((n_z, n_rows // 2, width), bf16),
            pltpu.VMEM((n_z - 1, n_rows, width), bf16),
            pltpu.VMEM((width, hidden_width), bf16),
            pltpu.VMEM((width, hidden_width), bf16),
            pltpu.VMEM((width, hidden_width), bf16),
            pltpu.SemaphoreType.DMA((messages,)),
            pltpu.SemaphoreType.DMA((messages,)),
            pltpu.SemaphoreType.DMA((3,)),
        ],
        compiler_params=pltpu.CompilerParams(
            collective_id=0, has_side_effects=True, vmem_limit_bytes=64 * 1024 * 1024 - 65536
        ),
    )(wide, w_gate[0], w_up[0], w_down[0].T)


def solution(mesh):
    def per_device(tokens, expert_ids, *others):
        n_exp = lax.axis_size("expert")
        if n_exp > 4 * expert_ids.shape[1]:
            return sparse_device(tokens, expert_ids, *others)
        paired = lax.axis_size("dp") == 4 and n_exp % 2 == 0 and tokens.shape[0] % 32 == 0
        return (fused_device if paired else dense_device)(tokens, expert_ids, *others)

    return jax.shard_map(
        per_device,
        mesh=mesh,
        in_specs=(
            P(("expert", "dp"), None),
            P(("expert", "dp"), None),
            P(("expert", "dp"), None),
            P("expert", None, "dp"),
            P("expert", None, "dp"),
            P("expert", "dp", None),
        ),
        out_specs=P(("expert", "dp"), None),
        check_vma=False,
    )
```

profile of v0, /device:TPU:0, one launch (start us, length us, event | category | flops | bytes accessed | tf_op | source)
XLA Modules:
  0.0 143.2 jit_solution(16579298684022932414)
XLA Ops:
  0.0 0.7 exponential_reduce_fusion
  0.7 0.7 exponential_divide_fusion
  1.4 0.7 select_reduce_fusion
  2.1 0.1 copy.12
  2.2 1.8 %fusion.1.wide_ref = bf16[64,2944]{1,0:T(8,128)(2,1)} fusion(bf16[64,16]{1,0:T(8,128)(2,1)S(1)} %copy.12, bf16[64,2880]{1,0:T(8,128)(2,1)} %param.6), kind=kLoop, calls=%fused_computation.2 | loop fusion | flops 1130496 | bytes 747520 | tf_op jit(solution)/shard_map/concatenate | solution.py:388
  4.0 137.4 %shard_map.64 = bf16[64,2880]{1,0:T(8,128)(2,1)} custom-call(bf16[64,2944]{1,0:T(8,128)(2,1)} %fusion.1.wide_ref, bf16[2880,384]{1,0:T(8,128)(2,1)} %bitcast.5, bf16[2880,384]{1,0:T(8,128)(2,1)} %bitcast.6, bf16[2880,384]{1,0:T(8,128)(2,1)} %bitcast.7), custom_call_target="tpu_custom_call" | custom-call | tf_op jit(solution)/shard_map/pallas_call | solution.py:394
  141.4 1.8 %copy.14 = bf16[64,2880]{1,0:T(8,128)(2,1)} copy(bf16[64,2880]{1,0:T(8,128)(2,1)} %shard_map.64) | data formatting | bytes 737280
  (2 shorter events, 0.0 us)
where the time goes:
time: 145 us; the launch traced here: 143 us
  Pallas kernels  137 us (94%)
  other arithmetic  3.91 us (3%)
  local copies, waits for them, and re-layouts  1.86 us (1%)
    pallas_call x1, Pallas kernels, fused_device(): pl.pallas_call(functools.partial(fused_kernel, n_exp), in_specs=[in_vmem,...  137 us

commit v1 on v0

--- a/solution.py
+++ b/solution.py
@@ -186,14 +186,17 @@
 
 
 def fused_kernel(
-    n_exp, wide_ref, gate_hbm, up_hbm, down_hbm, out_ref,
-    held, part, core_in, x_in, y_in, x_diag, y_diag, z_in,
+    n_exp, tok_hbm, ids_ref, logits_ref, gate_hbm, up_hbm, down_hbm, out_ref,
+    tok, held, part, core_in, x_in, y_in, x_diag, y_diag, d_chain, o_chain,
     gate_ref, up_ref, down_ref, send_sem, recv_sem, load_sem,
 ):
     n_z = n_exp // 2
+    reach = n_z // 2
     n_rows, width = out_ref.shape
-    lanes = wide_ref.shape[1]
-    half = n_rows // 2
+    lanes = held.shape[2]
+    rows = held.shape[1]
+    batches = n_rows // rows
+    half = rows // 2
     spare = width // LANES * LANES
     expert, dp = lax.axis_index("expert"), lax.axis_index("dp")
     z, y = lax.div(expert, 2), lax.rem(expert, 2)
@@ -201,35 +204,94 @@
     to_x = (expert, (1 - x) * 2 + core)
     to_y = (z * 2 + 1 - y, dp)
     to_core = (expert, x * 2 + 1 - core)
-
-    def at_z(d):
-        return lax.rem(z + d, n_z)
-
-    def to_z(d):
-        return (at_z(d) * 2 + y, dp)
-
     columns = {"o": y * 2 + x, "x": y * 2 + 1 - x, "y": (1 - y) * 2 + x, "d": (1 - y) * 2 + 1 - x}
-
-    def block(column, which, zz=0):
-        return (columns[column] * 2 + which) * n_z + zz
-
-    copies = {}
-
-    def start(key, source, target, device):
-        number = len(copies)
-        copies[key] = pltpu.make_async_remote_copy(
+    order = "oxyd"
+
+    def to_z(place):
+        return (place * 2 + y, dp)
+
+    short = jnp.minimum(z, n_z - 1 - z)
+    inward = jnp.where(z * 2 < n_z - 1, 1, -1)
+
+    def near(i):
+        if i == 0:
+            return z
+        paired = z - inward * ((i + 1) // 2) if i % 2 else z + inward * (i // 2)
+        return jnp.where(i <= 2 * short, paired, z + inward * (i - short))
+
+    class Plane:
+        def __init__(self, i):
+            self.i, self.zz = i, near(i)
+            self.dist = jnp.abs(self.zz - z)
+            self.away = jnp.where(self.zz < z, 1, -1)
+            self.out = z + self.away
+            self.back = z - self.away
+            self.has_out = (self.out >= 0) & (self.out < n_z)
+            self.maybe_far = i > reach
+            self.far = self.dist > reach
+            self.out_d = self.has_out & (self.dist < reach)
+
+    planes = [Plane(i) for i in range(n_z)]
+    others = range(1, n_z)
+
+    def block(column, which, zz, h):
+        return ((h * 4 + columns[column]) * 2 + which) * n_z + zz
+
+    kinds = {}
+    n_recv = [0]
+
+    def recv_index(kind, at):
+        if kind not in kinds:
+            size = RECV[kind](n_z, batches)
+            kinds[kind] = n_recv[0]
+            n_recv[0] += size
+        return kinds[kind] + at
+
+    for kind in RECV:
+        recv_index(kind, 0)
+
+    def at(kind, h, zz):
+        return recv_index(kind, h * n_z + zz)
+
+    def at_core(h, column, zz):
+        return recv_index("core", (h * 4 + order.index(column)) * n_z + zz)
+
+    def at_chain(kind, h, slot):
+        return recv_index(kind, h * (n_z + 1) + slot)
+
+    sent = []
+
+    def when(condition, action):
+        if condition is None:
+            action()
+        else:
+            pl.when(condition)(action)
+
+    def start(index, source, target, device, condition=None):
+        copy = pltpu.make_async_remote_copy(
             src_ref=source,
             dst_ref=target,
-            send_sem=send_sem.at[number],
-            recv_sem=recv_sem.at[number],
+            send_sem=send_sem.at[len(sent)],
+            recv_sem=recv_sem.at[index],
             device_id=device,
             device_id_type=pl.DeviceIdType.MESH,
         )
-        copies[key].start()
-
-    def arrived(*key):
-        copies[key].wait_recv()
-
+        sent.append((condition, copy))
+        when(condition, copy.start)
+
+    def arrived(index, target, condition=None):
+        copy = pltpu.make_async_remote_copy(
+            src_ref=target,
+            dst_ref=target,
+            send_sem=send_sem.at[0],
+            recv_sem=recv_sem.at[index],
+            device_id=to_core,
+            device_id_type=pl.DeviceIdType.MESH,
+        )
+        when(condition, copy.wait_recv)
+
+    tok_load = pltpu.make_async_copy(tok_hbm, tok, load_sem.at[3])
+    tok_load.start()
     loads = [
         pltpu.make_async_copy(source, target, load_sem.at[i])
         for i, (source, target) in enumerate(((gate_hbm, gate_ref), (up_hbm, up_ref), (down_hbm, down_ref)))
@@ -237,145 +299,335 @@
     for load in loads:
         load.start()
 
-    partners = [to_x, to_y, to_core] + [to_z(d) for d in range(1, n_z)]
+    above, below = z < n_z - 1, z > 0
     barrier = pltpu.get_barrier_semaphore()
-    for partner in partners:
-        pl.semaphore_signal(barrier, inc=1, device_id=partner, device_id_type=pl.DeviceIdType.MESH)
-    pl.semaphore_wait(barrier, len(partners))
-
-    near = sorted(range(1, n_z), key=lambda d: min(d, n_z - d))
-    own = held.at[block("o", core, z)]
-    start(("x", 0), wide_ref, own, to_x)
-    start(("y", 0), wide_ref, own, to_y)
-    for d in near:
-        start(("z", d), wide_ref, own, to_z(d))
-    start(("co", 0), wide_ref, own, to_core)
-    own[...] = wide_ref[...]
-
-    def relay_z(d):
-        arrived("z", d)
-        source = held.at[block("o", core, at_z(n_z - d))]
-        start(("x", d), source, source, to_x)
-        start(("y", d), source, source, to_y)
-        start(("co", d), source, source, to_core)
-
-    def relay_xy(d):
-        zz = at_z(n_z - d)
-        arrived("x", d)
-        source = held.at[block("x", core, zz)]
-        upper = held.at[block("x", core, zz), pl.ds(0, half)]
-        start(("y2", d), upper, upper, to_y)
-        start(("cx", d), source, source, to_core)
-        arrived("y", d)
-        source = held.at[block("y", core, zz)]
-        lower = held.at[block("y", core, zz), pl.ds(half, half)]
-        start(("x2", d), lower, lower, to_x)
-        start(("cy", d), source, source, to_core)
-
-    def relay_diag(d):
-        source = held.at[block("d", core, at_z(n_z - d))]
-        arrived("x2", d)
-        arrived("y2", d)
-        start(("cd", d), source, source, to_core)
-
-    def product(column, which):
-        span = pl.ds(block(column, which), n_z)
-        rows_in = held[span, :, :width].reshape(n_z * n_rows, width)
-        extra = held[span, :, spare:lanes].reshape(n_z * n_rows, lanes - spare)
-        result = tile_product(n_exp, rows_in, extra, gate_ref, up_ref, down_ref)
-        part[span] = result.astype(part.dtype).reshape(n_z, n_rows, width)
-
-    order = "oxyd"
-
-    def swap(column):
-        for d in range(n_z):
-            arrived("c" + column, d)
-        product(column, 1 - core)
-        start(("p", column), part.at[pl.ds(block(column, 1 - core), n_z)], core_in.at[order.index(column)], to_core)
-
-    def combine(column):
-        arrived("p", column)
-        place = order.index(column)
-        base = block(column, core)
-
-        @pl.loop(0, n_z)
-        def _(zz):
-            part[base + zz] = part[base + zz] + core_in[place, zz]
-
-    waiting = [0]
-    for d in near:
-        relay_z(d)
-        if d == near[-1]:
+
+    def greet(device):
+        pl.semaphore_signal(barrier, inc=1, device_id=device, device_id_type=pl.DeviceIdType.MESH)
+
+    for device in (to_x, to_y, to_core):
+        greet(device)
+    pl.when(above)(lambda: greet(to_z(z + 1)))
+    pl.when(below)(lambda: greet(to_z(z - 1)))
+
+    wts = jnp.exp(logits_ref[...])
+    wts = wts / jnp.sum(wts, axis=0, keepdims=True)
+    ids = ids_ref[...]
+    by_expert = jnp.concatenate(
+        [jnp.sum(jnp.where(ids == e, wts, 0.0), axis=0, keepdims=True) for e in range(n_exp)], axis=0
+    )
+    high = by_expert.astype(jnp.bfloat16).astype(jnp.float32)
+    pairs = jnp.concatenate([high, by_expert - high], axis=0)
+    filled = jnp.concatenate(
+        [pairs, jnp.zeros((lanes - width - pairs.shape[0], n_rows), jnp.float32)], axis=0
+    ).astype(jnp.bfloat16)
+    eye = (
+        lax.broadcasted_iota(jnp.int32, (n_rows, n_rows), 0)
+        == lax.broadcasted_iota(jnp.int32, (n_rows, n_rows), 1)
+    ).astype(jnp.float32).astype(jnp.bfloat16)
+    extra_cols = lax.dot_general(
+        eye, filled, (((1,), (1,)), ((), ())), preferred_element_type=jnp.float32
+    ).astype(jnp.bfloat16)
+    tok_load.wait()
+    for h in range(batches):
+        own = block("o", core, z, h)
+        held[own, :, :width] = tok[h * rows : (h + 1) * rows]
+        held[own, :, width:] = extra_cols[h * rows : (h + 1) * rows]
+    pl.semaphore_wait(barrier, 3 + above.astype(jnp.int32) + below.astype(jnp.int32))
+
+    def send_own(h):
+        own = held.at[block("o", core, z, h)]
+        start(at("x", h, z), own, own, to_x)
+        start(at("y", h, z), own, own, to_y)
+        start(at("o", h, z), own, own, to_z(z + 1), above)
+        start(at("o", h, z), own, own, to_z(z - 1), below)
+        start(at_core(h, "o", z), own, own, to_core)
+
+    def take_x(h, i):
+        p = planes[i]
+        spot = block("x", core, p.zz, h)
+        arrived(at("x", h, p.zz), held.at[spot])
+        upper = held.at[spot, pl.ds(0, half)]
+        if i == 0 or p.maybe_far:
+            start(at("y2", h, p.zz), upper, upper, to_y, p.far if i else None)
+        start(at_core(h, "x", p.zz), held.at[spot], held.at[spot], to_core)
+
+    def take_y(h, i):
+        p = planes[i]
+        spot = block("y", core, p.zz, h)
+        arrived(at("y", h, p.zz), held.at[spot])
+        lower = held.at[spot, pl.ds(half, half)]
+        if i == 0 or p.maybe_far:
+            start(at("x2", h, p.zz), lower, lower, to_x, p.far if i else None)
+        start(at_core(h, "y", p.zz), held.at[spot], held.at[spot], to_core)
+
+    def take_xy(h, i):
+        take_x(h, i)
+        take_y(h, i)
+
+    def take_o(h, i):
+        p = planes[i]
+        spot = held.at[block("o", core, p.zz, h)]
+        arrived(at("o", h, p.zz), spot)
+        start(at("o", h, p.zz), spot, spot, to_z(p.out), p.has_out)
+        start(at("x", h, p.zz), spot, spot, to_x)
+        start(at("y", h, p.zz), spot, spot, to_y)
+        start(at_core(h, "o", p.zz), spot, spot, to_core)
+
+    def take_d(h, i):
+        p = planes[i]
+        index = block("d", core, p.zz, h)
+        spot = held.at[index]
+
+        def halves(condition):
+            arrived(at("x2", h, p.zz), held.at[index, pl.ds(half, half)], condition)
+            arrived(at("y2", h, p.zz), held.at[index, pl.ds(0, half)], condition)
+
+        if i == 0:
+            halves(None)
+            start(at("d", h, z), spot, spot, to_z(z + 1), above)
+            start(at("d", h, z), spot, spot, to_z(z - 1), below)
+        else:
+            if p.maybe_far:
+                halves(p.far)
+            arrived(at("d", h, p.zz), spot, p.dist <= reach if p.maybe_far else None)
+            start(at("d", h, p.zz), spot, spot, to_z(p.out), p.out_d)
+        start(at_core(h, "d", p.zz), spot, spot, to_core)
+
+    loaded = []
+
+    def product(h, column):
+        for zz in range(n_z):
+            arrived(at_core(h, column, zz), held.at[block(column, 1 - core, zz, h)])
+        if not loaded:
             for load in loads:
                 load.wait()
-            product("o", core)
-        relay_xy(waiting.pop())
-        waiting.append(d)
-    swap("o")
-    relay_xy(waiting.pop())
-    product("x", core)
-    swap("x")
-    relay_diag(0)
-    product("y", core)
-    for d in near[:-1]:
-        relay_diag(d)
-    combine("x")
-    rows_x = pl.ds(block("x", core), n_z)
-    start(("ex",), part.at[rows_x, pl.ds(half, half)], x_in.at[:, pl.ds(half, half)], to_x)
-    swap("y")
-    relay_diag(near[-1])
-    product("d", core)
-    combine("y")
-    rows_y = pl.ds(block("y", core), n_z)
-    start(("ey",), part.at[rows_y, pl.ds(0, half)], y_in.at[:, pl.ds(0, half)], to_y)
-    swap("d")
-    combine("d")
-    far = near[::-1] + [0]
-    for d in far:
-        source = block("d", core, at_z(d))
-        start(("dx", d), part.at[source, pl.ds(half, half)], x_diag.at[d], to_x)
-        start(("dy", d), part.at[source, pl.ds(0, half)], y_diag.at[d], to_y)
-    combine("o")
-
-    def gather_diag(d):
-        zz = at_z(d)
-        arrived("dx", d)
-        spot = block("y", core, zz)
-        part[spot, half:] = part[spot, half:] + x_diag[d]
-        start(("fy", d), part.at[spot, pl.ds(half, half)], y_in.at[zz, pl.ds(half, half)], to_y)
-        arrived("dy", d)
-        spot = block("x", core, zz)
-        part[spot, :half] = part[spot, :half] + y_diag[d]
-        start(("fx", d), part.at[spot, pl.ds(0, half)], x_in.at[zz, pl.ds(0, half)], to_x)
-
-    def gather_xy(d):
-        zz = at_z(d)
-        arrived("fx", d)
-        arrived("fy", d)
-        total = (
-            part[block("o", core, zz)].astype(jnp.float32)
-            + x_in[zz].astype(jnp.float32)
-            + y_in[zz].astype(jnp.float32)
+            loaded.append(True)
+        span = pl.ds(block(column, 0, 0, h), 2 * n_z)
+        rows_in = held[span, :, :width].reshape(2 * n_z * rows, width)
+        extra = held[span, :, spare:lanes].reshape(2 * n_z * rows, lanes - spare)
+        result = tile_product(n_exp, rows_in, extra, gate_ref, up_ref, down_ref)
+        part[span] = result.astype(part.dtype).reshape(2 * n_z, rows, width)
+        start(
+            recv_index("p", h * 4 + order.index(column)),
+            part.at[pl.ds(block(column, 1 - core, 0, h), n_z)],
+            core_in.at[pl.ds((h * 4 + order.index(column)) * n_z, n_z)],
+            to_core,
         )
-        if d == 0:
-            for other in far[:-1]:
-                arrived("s", other)
-                total = total + z_in[other - 1].astype(jnp.float32)
-            out_ref[...] = total.astype(out_ref.dtype)
+
+    def chained(chain, slot):
+        chain[slot] = jnp.zeros(chain.shape[1:], chain.dtype)
+
+    def clear():
+        for h in range(batches):
+            base = h * (n_z + 1)
+            for p in planes[1:]:
+                missing = (p.back < 0) | (p.back >= n_z)
+                flipped = z + p.away
+                no_up = (flipped < 0) | (flipped >= n_z)
+                pl.when(no_up)(lambda p=p, base=base: chained(o_chain, base + p.zz))
+                pl.when(no_up | (p.dist >= reach))(lambda p=p, base=base: chained(d_chain, base + p.zz))
+                if p.maybe_far:
+
+                    @pl.when(jnp.logical_not(p.far))
+                    def _(p=p, h=h):
+                        chained(x_diag, h * n_z + p.zz)
+                        chained(y_diag, h * n_z + p.zz)
+
+            for chain in (o_chain, d_chain):
+                pl.when(z == 0)(lambda chain=chain, base=base: chained(chain, base + z))
+                pl.when(z == n_z - 1)(lambda chain=chain, base=base: chained(chain, base + n_z))
+
+    step = 16 if half % 16 == 0 else half
+
+    def combined(h, column, zz, *more, target=None):
+        spot = block(column, core, zz, h)
+        place = (h * 4 + order.index(column)) * n_z + zz
+
+        @pl.loop(0, rows // step)
+        def _(k):
+            span = pl.ds(k * step, step)
+            total = part[spot, span].astype(jnp.float32) + core_in[place, span].astype(jnp.float32)
+            for source, index in more:
+                total = total + source[index, span].astype(jnp.float32)
+            if target is None:
+                part[spot, span] = total.astype(part.dtype)
+            else:
+                out_ref[pl.ds(target + k * step, step)] = total.astype(out_ref.dtype)
+
+        return spot
+
+    seen = set()
+
+    def need(h, column):
+        if (h, column) not in seen:
+            seen.add((h, column))
+            base = (h * 4 + order.index(column)) * n_z
+            arrived(recv_index("p", h * 4 + order.index(column)), core_in.at[pl.ds(base, n_z)])
+
+    def slot_at(p):
+        toward = z - p.away
+        return jnp.where((toward == p.zz) & (p.away > 0), n_z, p.zz)
+
+    def give_d(h, i):
+        p = planes[i]
+        base = h * (n_z + 1)
+        need(h, "d")
+        if i == 0:
+            arrived(at_chain("dc", h, z), d_chain.at[base + z], below)
+            arrived(at_chain("dc", h, n_z), d_chain.at[base + n_z], above)
+            spot = combined(h, "d", z, (d_chain, base + z), (d_chain, base + n_z))
         else:
-            spot = block("o", core, zz)
-            part[spot] = total.astype(part.dtype)
-            start(("s", d), part.at[spot], z_in.at[d - 1], to_z(d))
-
-    gather_diag(far[0])
-    arrived("ex")
-    arrived("ey")
-    for before, d in zip(far, far[1:]):
-        gather_diag(d)
-        gather_xy(before)
-    gather_xy(far[-1])
-    for copy in copies.values():
-        copy.wait_send()
+            has_up = p.has_out & (p.dist < reach)
+            arrived(at_chain("dc", h, p.zz), d_chain.at[base + p.zz], has_up)
+            spot = combined(h, "d", p.zz, (d_chain, base + p.zz))
+            start(
+                at_chain("dc", h, slot_at(p)), part.at[spot], d_chain.at[base + slot_at(p)], to_z(p.back),
+                jnp.logical_not(p.far) if p.maybe_far else None,
+            )
+        if i == 0 or p.maybe_far:
+            condition = p.far if i else None
+            start(at("dx", h, p.zz), part.at[spot, pl.ds(half, half)], x_diag.at[h * n_z + p.zz], to_x, condition)
+            start(at("dy", h, p.zz), part.at[spot, pl.ds(0, half)], y_diag.at[h * n_z + p.zz], to_y, condition)
+
+    def give_x(h, i):
+        p = planes[i]
+        need(h, "x")
+        index = h * n_z + p.zz
+        spot = combined(h, "x", p.zz)
+        if i == 0 or p.maybe_far:
+            arrived(at("dy", h, p.zz), y_diag.at[index], p.far if i else None)
+            part[spot, :half] = (
+                part[spot, :half].astype(jnp.float32) + y_diag[index].astype(jnp.float32)
+            ).astype(part.dtype)
+        start(at("rx", h, p.zz), part.at[spot], x_in.at[index], to_x)
+
+    def give_y(h, i):
+        p = planes[i]
+        need(h, "y")
+        index = h * n_z + p.zz
+        spot = combined(h, "y", p.zz)
+        if i == 0 or p.maybe_far:
+            arrived(at("dx", h, p.zz), x_diag.at[index], p.far if i else None)
+            part[spot, half:] = (
+                part[spot, half:].astype(jnp.float32) + x_diag[index].astype(jnp.float32)
+            ).astype(part.dtype)
+        start(at("ry", h, p.zz), part.at[spot], y_in.at[index], to_y)
+
+    def give_xy(h, i):
+        give_x(h, i)
+        give_y(h, i)
+
+    def give_o(h, i):
+        p = planes[i]
+        base = h * (n_z + 1)
+        index = h * n_z + p.zz
+        need(h, "o")
+        arrived(at("rx", h, p.zz), x_in.at[index])
+        arrived(at("ry", h, p.zz), y_in.at[index])
+        if i == 0:
+            arrived(at_chain("oc", h, z), o_chain.at[base + z], below)
+            arrived(at_chain("oc", h, n_z), o_chain.at[base + n_z], above)
+            combined(
+                h, "o", z, (x_in, index), (y_in, index), (o_chain, base + z), (o_chain, base + n_z),
+                target=h * rows,
+            )
+        else:
+            arrived(at_chain("oc", h, p.zz), o_chain.at[base + p.zz], p.has_out)
+            spot = combined(h, "o", p.zz, (x_in, index), (y_in, index), (o_chain, base + p.zz))
+            start(at_chain("oc", h, slot_at(p)), part.at[spot], o_chain.at[base + slot_at(p)], to_z(p.back))
+
+    steps = {
+        "own": send_own, "clear": clear, "x": take_x, "y": take_y, "xy": take_xy, "o": take_o, "d": take_d,
+        "C": product, "Rd": give_d, "Rx": give_x, "Ry": give_y, "Rxy": give_xy, "Ro": give_o,
+    }
+    for name, *numbers in PLAN:
+        steps[name](*numbers)
+    for condition, copy in sent:
+        when(condition, copy.wait_send)
+
+
+RECV = {kind: (lambda n_z, batches: n_z * batches) for kind in ("x", "y", "o", "d", "x2", "y2", "dx", "dy", "rx", "ry")}
+RECV["core"] = lambda n_z, batches: 4 * n_z * batches
+RECV["p"] = lambda n_z, batches: 4 * batches
+RECV["dc"] = RECV["oc"] = lambda n_z, batches: (n_z + 1) * batches
+
+
+PLAN = (
+    ("own", 0),
+    ("own", 1),
+    ("x", 0, 0),
+    ("clear",),
+    ("y", 0, 0),
+    ("o", 0, 1),
+    ("o", 0, 2),
+    ("x", 1, 0),
+    ("y", 1, 0),
+    ("d", 0, 0),
+    ("o", 0, 3),
+    ("o", 1, 1),
+    ("x", 0, 2),
+    ("x", 0, 1),
+    ("y", 0, 1),
+    ("d", 0, 2),
+    ("d", 0, 1),
+    ("C", 0, "o"),
+    ("x", 0, 3),
+    ("y", 0, 3),
+    ("o", 1, 3),
+    ("d", 0, 3),
+    ("C", 0, "x"),
+    ("o", 1, 2),
+    ("d", 1, 0),
+    ("y", 0, 2),
+    ("y", 1, 1),
+    ("C", 0, "d"),
+    ("x", 1, 3),
+    ("x", 1, 1),
+    ("y", 1, 3),
+    ("C", 0, "y"),
+    ("Rx", 0, 2),
+    ("Rd", 0, 3),
+    ("x", 1, 2),
+    ("d", 1, 2),
+    ("d", 1, 1),
+    ("Rd", 0, 2),
+    ("d", 1, 3),
+    ("Ry", 0, 1),
+    ("y", 1, 2),
+    ("Rx", 0, 1),
+    ("Rd", 0, 1),
+    ("Ry", 0, 2),
+    ("C", 1, "d"),
+    ("C", 1, "x"),
+    ("Rd", 1, 3),
+    ("Ry", 0, 3),
+    ("Rd", 1, 2),
+    ("Rx", 0, 3),
+    ("C", 1, "y"),
+    ("Ro", 0, 2),
+    ("Rd", 0, 0),
+    ("Rx", 1, 3),
+    ("Rx", 1, 2),
+    ("Rd", 1, 1),
+    ("Ry", 1, 3),
+    ("Rx", 1, 1),
+    ("Ry", 1, 2),
+    ("Ro", 0, 3),
+    ("Ry", 1, 1),
+    ("C", 1, "o"),
+    ("Ro", 1, 3),
+    ("Rd", 1, 0),
+    ("Ry", 0, 0),
+    ("Rx", 0, 0),
+    ("Ro", 1, 2),
+    ("Ro", 0, 1),
+    ("Rx", 1, 0),
+    ("Ro", 1, 1),
+    ("Ry", 1, 0),
+    ("Ro", 0, 0),
+    ("Ro", 1, 0),
+)
 
 
 def fused_device(tokens, expert_ids, gate_logits, w_gate, w_up, w_down):
@@ -383,39 +635,42 @@
     hidden_width = w_gate.shape[2]
     n_exp = lax.axis_size("expert")
     n_z = n_exp // 2
+    batches = 2
+    rows = n_rows // batches
     lanes = round_up(width + 2 * n_exp, LANES)
-    extra = routing_columns(expert_ids, gate_logits, n_exp, lanes - width)
-    wide = jnp.concatenate([tokens, extra], axis=1)
-    total = n_exp * lax.axis_size("dp")
-    messages = 8 * n_z + 4 * n_z + 4 + 2 + 4 * n_z + n_z + n_z
+    total = n_exp * lax.axis_size("dp") * batches
+    receives = sum(size(n_z, batches) for size in RECV.values())
+    sends = 64 * n_z
     bf16 = jnp.bfloat16
     in_vmem = pl.BlockSpec(memory_space=pltpu.VMEM)
     anywhere = pl.BlockSpec(memory_space=pl.ANY)
     return pl.pallas_call(
         functools.partial(fused_kernel, n_exp),
-        in_specs=[in_vmem, anywhere, anywhere, anywhere],
+        in_specs=[anywhere, in_vmem, in_vmem, anywhere, anywhere, anywhere],
         out_specs=in_vmem,
         out_shape=jax.ShapeDtypeStruct((n_rows, width), bf16),
         scratch_shapes=[
-            pltpu.VMEM((total, n_rows, lanes), bf16),
-            pltpu.VMEM((total, n_rows, width), bf16),
-            pltpu.VMEM((4, n_z, n_rows, width), bf16),
-            pltpu.VMEM((n_z, n_rows, width), bf16),
-            pltpu.VMEM((n_z, n_rows, width), bf16),
-            pltpu.VMEM((n_z, n_rows // 2, width), bf16),
-            pltpu.VMEM((n_z, n_rows // 2, width), bf16),
-            pltpu.VMEM((n_z - 1, n_rows, width), bf16),
+            pltpu.VMEM((n_rows, width), bf16),
+            pltpu.VMEM((total, rows, lanes), bf16),
+            pltpu.VMEM((total, rows, width), bf16),
+            pltpu.VMEM((total // 2, rows, width), bf16),
+            pltpu.VMEM((batches * n_z, rows, width), bf16),
+            pltpu.VMEM((batches * n_z, rows, width), bf16),
+            pltpu.VMEM((batches * n_z, rows // 2, width), bf16),
+            pltpu.VMEM((batches * n_z, rows // 2, width), bf16),
+            pltpu.VMEM((batches * (n_z + 1), rows, width), bf16),
+            pltpu.VMEM((batches * (n_z + 1), rows, width), bf16),
             pltpu.VMEM((width, hidden_width), bf16),
             pltpu.VMEM((width, hidden_width), bf16),
             pltpu.VMEM((width, hidden_width), bf16),
-            pltpu.SemaphoreType.DMA((messages,)),
-            pltpu.SemaphoreType.DMA((messages,)),
-            pltpu.SemaphoreType.DMA((3,)),
+            pltpu.SemaphoreType.DMA((sends,)),
+            pltpu.SemaphoreType.DMA((receives,)),
+            pltpu.SemaphoreType.DMA((4,)),
         ],
         compiler_params=pltpu.CompilerParams(
             collective_id=0, has_side_effects=True, vmem_limit_bytes=64 * 1024 * 1024 - 65536
         ),
-    )(wide, w_gate[0], w_up[0], w_down[0].T)
+    )(tokens, expert_ids.T, gate_logits.T, w_gate[0], w_up[0], w_down[0].T)
 
 
 def solution(mesh):

time: 145 us -> 100 us (0.69); the launches traced: 143 us -> 99.9 us
  Pallas kernels: 137 us -> 98.1 us
  other arithmetic: 3.91 us -> 0 us
    pallas_call x1, Pallas kernels: 137 us -> 98.1 us  [fused_device(): pl.pallas_call(functools.partial(fused_kernel, n_exp), in_specs=[anywhere...]
    concatenate x2 -> x0, other arithmetic: 1.82 us -> none  [the longest x1 1.81 us: fused_device(): wide = jnp.concatenate([tokens, extra], axis=1)]
where the time goes in v1:
time: 100 us; the launch traced here: 99.9 us
  Pallas kernels  98.1 us (98%)
  local copies, waits for them, and re-layouts  1.76 us (2%)
    pallas_call x1, Pallas kernels, fused_device(): pl.pallas_call(functools.partial(fused_kernel, n_exp), in_specs=[anywhere...  98.1 us

profile of v1, /device:TPU:0, one launch (start us, length us, event | category | flops | bytes accessed | tf_op | source)
XLA Modules:
  0.0 99.9 jit_solution(5051323729283966889)
XLA Ops:
  0.0 98.1 %shard_map.64 = bf16[64,2880]{1,0:T(8,128)(2,1)} custom-call(bf16[64,2880]{1,0:T(8,128)(2,1)} %tok_hbm.1, s32[4,64]{1,0:T(4,128)} %bitcast.10, f32[4,64]{1,0:T(4,128)} %bitcast.11, bf16[2880,384]{1,0:T(8,128)(2,1)} %bitcast.7, bf16[2880,384]{1,0:T(8,128)(2,1)} %bitcast.8, bf16[2880,384]{1,0:T(8,128)(2,1)} %bitcast.9), custom_call_target="tpu_custom_call" | custom-call | tf_op jit(solution)/shard_map/pallas_call | solution.py:647
  98.1 1.8 %copy.8 = bf16[64,2880]{1,0:T(8,128)(2,1)} copy(bf16[64,2880]{1,0:T(8,128)(2,1)} %shard_map.64) | data formatting | bytes 737280

commit v2 on v1

--- a/solution.py
+++ b/solution.py
@@ -186,8 +186,8 @@
 
 
 def fused_kernel(
-    n_exp, tok_hbm, ids_ref, logits_ref, gate_hbm, up_hbm, down_hbm, out_ref,
-    tok, held, part, core_in, x_in, y_in, x_diag, y_diag, d_chain, o_chain,
+    n_exp, tok_hbm, ids_hbm, logits_hbm, gate_hbm, up_hbm, down_hbm, out_ref,
+    ids_ref, logits_ref, tok, held, part, core_in, x_in, y_in, x_diag, y_diag, d_chain, o_chain,
     gate_ref, up_ref, down_ref, send_sem, recv_sem, load_sem,
 ):
     n_z = n_exp // 2
@@ -290,15 +290,6 @@
         )
         when(condition, copy.wait_recv)
 
-    tok_load = pltpu.make_async_copy(tok_hbm, tok, load_sem.at[3])
-    tok_load.start()
-    loads = [
-        pltpu.make_async_copy(source, target, load_sem.at[i])
-        for i, (source, target) in enumerate(((gate_hbm, gate_ref), (up_hbm, up_ref), (down_hbm, down_ref)))
-    ]
-    for load in loads:
-        load.start()
-
     above, below = z < n_z - 1, z > 0
     barrier = pltpu.get_barrier_semaphore()
 
@@ -310,6 +301,18 @@
     pl.when(above)(lambda: greet(to_z(z + 1)))
     pl.when(below)(lambda: greet(to_z(z - 1)))
 
+    small = [
+        pltpu.make_async_copy(source, target, load_sem.at[i])
+        for i, (source, target) in enumerate(((ids_hbm, ids_ref), (logits_hbm, logits_ref), (tok_hbm, tok)))
+    ]
+    for load in small:
+        load.start()
+    loads = [
+        pltpu.make_async_copy(source, target, load_sem.at[3 + i])
+        for i, (source, target) in enumerate(((gate_hbm, gate_ref), (up_hbm, up_ref), (down_hbm, down_ref)))
+    ]
+    small[0].wait()
+    small[1].wait()
     wts = jnp.exp(logits_ref[...])
     wts = wts / jnp.sum(wts, axis=0, keepdims=True)
     ids = ids_ref[...]
@@ -328,7 +331,9 @@
     extra_cols = lax.dot_general(
         eye, filled, (((1,), (1,)), ((), ())), preferred_element_type=jnp.float32
     ).astype(jnp.bfloat16)
-    tok_load.wait()
+    small[2].wait()
+    for load in loads:
+        load.start()
     for h in range(batches):
         own = block("o", core, z, h)
         held[own, :, :width] = tok[h * rows : (h + 1) * rows]
@@ -438,7 +443,7 @@
                 pl.when(z == 0)(lambda chain=chain, base=base: chained(chain, base + z))
                 pl.when(z == n_z - 1)(lambda chain=chain, base=base: chained(chain, base + n_z))
 
-    step = 16 if half % 16 == 0 else half
+    step = 16 if rows % 16 == 0 else rows
 
     def combined(h, column, zz, *more, target=None):
         spot = block(column, core, zz, h)
@@ -553,11 +558,13 @@
 RECV["dc"] = RECV["oc"] = lambda n_z, batches: (n_z + 1) * batches
 
 
+BATCHES = 2
+
 PLAN = (
     ("own", 0),
+    ("clear",),
     ("own", 1),
     ("x", 0, 0),
-    ("clear",),
     ("y", 0, 0),
     ("o", 0, 1),
     ("o", 0, 2),
@@ -565,65 +572,65 @@
     ("y", 1, 0),
     ("d", 0, 0),
     ("o", 0, 3),
+    ("y", 0, 1),
     ("o", 1, 1),
+    ("x", 0, 1),
+    ("C", 0, "o"),
+    ("y", 0, 2),
+    ("d", 0, 1),
+    ("d", 0, 2),
     ("x", 0, 2),
-    ("x", 0, 1),
-    ("y", 0, 1),
-    ("d", 0, 2),
-    ("d", 0, 1),
-    ("C", 0, "o"),
+    ("y", 0, 3),
     ("x", 0, 3),
-    ("y", 0, 3),
     ("o", 1, 3),
     ("d", 0, 3),
-    ("C", 0, "x"),
+    ("C", 0, "y"),
     ("o", 1, 2),
     ("d", 1, 0),
-    ("y", 0, 2),
     ("y", 1, 1),
     ("C", 0, "d"),
+    ("y", 1, 3),
     ("x", 1, 3),
-    ("x", 1, 1),
-    ("y", 1, 3),
-    ("C", 0, "y"),
-    ("Rx", 0, 2),
+    ("C", 0, "x"),
     ("Rd", 0, 3),
-    ("x", 1, 2),
+    ("Ry", 0, 2),
+    ("Ry", 0, 1),
     ("d", 1, 2),
     ("d", 1, 1),
     ("Rd", 0, 2),
     ("d", 1, 3),
-    ("Ry", 0, 1),
-    ("y", 1, 2),
     ("Rx", 0, 1),
     ("Rd", 0, 1),
-    ("Ry", 0, 2),
+    ("x", 1, 2),
+    ("y", 1, 2),
+    ("Rx", 0, 2),
+    ("x", 1, 1),
     ("C", 1, "d"),
+    ("Rx", 0, 3),
     ("C", 1, "x"),
     ("Rd", 1, 3),
+    ("Rd", 1, 2),
     ("Ry", 0, 3),
-    ("Rd", 1, 2),
-    ("Rx", 0, 3),
     ("C", 1, "y"),
     ("Ro", 0, 2),
     ("Rd", 0, 0),
     ("Rx", 1, 3),
     ("Rx", 1, 2),
+    ("Rx", 1, 1),
     ("Rd", 1, 1),
     ("Ry", 1, 3),
-    ("Rx", 1, 1),
     ("Ry", 1, 2),
-    ("Ro", 0, 3),
     ("Ry", 1, 1),
     ("C", 1, "o"),
+    ("Ro", 0, 3),
     ("Ro", 1, 3),
     ("Rd", 1, 0),
+    ("Rx", 0, 0),
     ("Ry", 0, 0),
-    ("Rx", 0, 0),
     ("Ro", 1, 2),
     ("Ro", 0, 1),
+    ("Ro", 1, 1),
     ("Rx", 1, 0),
-    ("Ro", 1, 1),
     ("Ry", 1, 0),
     ("Ro", 0, 0),
     ("Ro", 1, 0),
@@ -635,7 +642,7 @@
     hidden_width = w_gate.shape[2]
     n_exp = lax.axis_size("expert")
     n_z = n_exp // 2
-    batches = 2
+    batches = BATCHES
     rows = n_rows // batches
     lanes = round_up(width + 2 * n_exp, LANES)
     total = n_exp * lax.axis_size("dp") * batches
@@ -646,10 +653,12 @@
     anywhere = pl.BlockSpec(memory_space=pl.ANY)
     return pl.pallas_call(
         functools.partial(fused_kernel, n_exp),
-        in_specs=[anywhere, in_vmem, in_vmem, anywhere, anywhere, anywhere],
+        in_specs=[anywhere] * 6,
         out_specs=in_vmem,
-        out_shape=jax.ShapeDtypeStruct((n_rows, width), bf16),
+        out_shape=pltpu.VMEM((n_rows, width), bf16),
         scratch_shapes=[
+            pltpu.VMEM(expert_ids.shape[::-1], jnp.int32),
+            pltpu.VMEM(gate_logits.shape[::-1], jnp.float32),
             pltpu.VMEM((n_rows, width), bf16),
             pltpu.VMEM((total, rows, lanes), bf16),
             pltpu.VMEM((total, rows, width), bf16),
@@ -665,10 +674,10 @@
             pltpu.VMEM((width, hidden_width), bf16),
             pltpu.SemaphoreType.DMA((sends,)),
             pltpu.SemaphoreType.DMA((receives,)),
-            pltpu.SemaphoreType.DMA((4,)),
+            pltpu.SemaphoreType.DMA((6,)),
         ],
         compiler_params=pltpu.CompilerParams(
-            collective_id=0, has_side_effects=True, vmem_limit_bytes=64 * 1024 * 1024 - 65536
+            collective_id=0, has_side_effects=True, vmem_limit_bytes=60 * 1024 * 1024
         ),
     )(tokens, expert_ids.T, gate_logits.T, w_gate[0], w_up[0], w_down[0].T)
 

time: 100 us -> 96.5 us (0.965)
  Pallas kernels: 98.1 us -> 95.5 us
  local copies, waits for them, and re-layouts: 1.76 us -> 0.74 us
    pallas_call x1, Pallas kernels: 98.1 us -> 95.5 us  [fused_device(): pl.pallas_call(functools.partial(fused_kernel, n_exp), in_specs=[anywhere...]
    unnamed x1, local copies, waits for them, and re-layouts: 1.76 us -> 0.74 us
where the time goes in v2:
time: 96.5 us; the launch traced here: 96.3 us
  Pallas kernels  95.5 us (99%)
    pallas_call x1, Pallas kernels, fused_device(): pl.pallas_call(functools.partial(fused_kernel, n_exp), in_specs=[anywhere...  95.5 us

profile of v2, /device:TPU:0, one launch (start us, length us, event | category | flops | bytes accessed | tf_op | source)
XLA Modules:
  0.0 96.3 jit_solution(1294483046113270863)
XLA Ops:
  0.0 95.5 %shard_map.64 = bf16[64,2880]{1,0:T(8,128)(2,1)S(1)} custom-call(bf16[64,2880]{1,0:T(8,128)(2,1)} %tok_hbm.1, s32[4,64]{1,0:T(4,128)} %bitcast.10, f32[4,64]{1,0:T(4,128)} %bitcast.11, bf16[2880,384]{1,0:T(8,128)(2,1)} %bitcast.7, bf16[2880,384]{1,0:T(8,128)(2,1)} %bitcast.8, bf16[2880,384]{1,0:T(8,128)(2,1)} %bitcast.9), custom_call_target="tpu_custom_call" | custom-call | tf_op jit(solution)/shard_map/pallas_call | solution.py:654
  95.6 0.7 copy.8

commit v3 on v2

--- a/solution.py
+++ b/solution.py
@@ -187,7 +187,7 @@
 
 def fused_kernel(
     n_exp, tok_hbm, ids_hbm, logits_hbm, gate_hbm, up_hbm, down_hbm, out_ref,
-    ids_ref, logits_ref, tok, held, part, core_in, x_in, y_in, x_diag, y_diag, d_chain, o_chain,
+    ids_ref, logits_ref, tok, held, part, core_in, sides_in, x_diag, y_diag, d_chain, o_chain,
     gate_ref, up_ref, down_ref, send_sem, recv_sem, load_sem,
 ):
     n_z = n_exp // 2
@@ -253,8 +253,11 @@
     def at(kind, h, zz):
         return recv_index(kind, h * n_z + zz)
 
-    def at_core(h, column, zz):
-        return recv_index("core", (h * 4 + order.index(column)) * n_z + zz)
+    def at_core(h, column):
+        return recv_index("core", h * 4 + order.index(column))
+
+    def at_far(kind, h, i):
+        return recv_index(kind, h * (n_z - reach) + (i - reach if i else 0))
 
     def at_chain(kind, h, slot):
         return recv_index(kind, h * (n_z + 1) + slot)
@@ -268,10 +271,13 @@
             pl.when(condition)(action)
 
     def start(index, source, target, device, condition=None):
+        if len(sent) >= SENDS:
+            before, oldest = sent[-SENDS]
+            when(before, oldest.wait_send)
         copy = pltpu.make_async_remote_copy(
             src_ref=source,
             dst_ref=target,
-            send_sem=send_sem.at[len(sent)],
+            send_sem=send_sem.at[len(sent) % SENDS],
             recv_sem=recv_sem.at[index],
             device_id=device,
             device_id_type=pl.DeviceIdType.MESH,
@@ -346,7 +352,7 @@
         start(at("y", h, z), own, own, to_y)
         start(at("o", h, z), own, own, to_z(z + 1), above)
         start(at("o", h, z), own, own, to_z(z - 1), below)
-        start(at_core(h, "o", z), own, own, to_core)
+        start(at_core(h, "o"), own, own, to_core)
 
     def take_x(h, i):
         p = planes[i]
@@ -354,8 +360,8 @@
         arrived(at("x", h, p.zz), held.at[spot])
         upper = held.at[spot, pl.ds(0, half)]
         if i == 0 or p.maybe_far:
-            start(at("y2", h, p.zz), upper, upper, to_y, p.far if i else None)
-        start(at_core(h, "x", p.zz), held.at[spot], held.at[spot], to_core)
+            start(at_far("halves", h, i), upper, upper, to_y, p.far if i else None)
+        start(at_core(h, "x"), held.at[spot], held.at[spot], to_core)
 
     def take_y(h, i):
         p = planes[i]
@@ -363,8 +369,8 @@
         arrived(at("y", h, p.zz), held.at[spot])
         lower = held.at[spot, pl.ds(half, half)]
         if i == 0 or p.maybe_far:
-            start(at("x2", h, p.zz), lower, lower, to_x, p.far if i else None)
-        start(at_core(h, "y", p.zz), held.at[spot], held.at[spot], to_core)
+            start(at_far("halves", h, i), lower, lower, to_x, p.far if i else None)
+        start(at_core(h, "y"), held.at[spot], held.at[spot], to_core)
 
     def take_xy(h, i):
         take_x(h, i)
@@ -377,33 +383,28 @@
         start(at("o", h, p.zz), spot, spot, to_z(p.out), p.has_out)
         start(at("x", h, p.zz), spot, spot, to_x)
         start(at("y", h, p.zz), spot, spot, to_y)
-        start(at_core(h, "o", p.zz), spot, spot, to_core)
+        start(at_core(h, "o"), spot, spot, to_core)
 
     def take_d(h, i):
         p = planes[i]
         index = block("d", core, p.zz, h)
         spot = held.at[index]
 
-        def halves(condition):
-            arrived(at("x2", h, p.zz), held.at[index, pl.ds(half, half)], condition)
-            arrived(at("y2", h, p.zz), held.at[index, pl.ds(0, half)], condition)
-
         if i == 0:
-            halves(None)
+            arrived(at_far("halves", h, i), spot)
             start(at("d", h, z), spot, spot, to_z(z + 1), above)
             start(at("d", h, z), spot, spot, to_z(z - 1), below)
         else:
             if p.maybe_far:
-                halves(p.far)
+                arrived(at_far("halves", h, i), spot, p.far)
             arrived(at("d", h, p.zz), spot, p.dist <= reach if p.maybe_far else None)
             start(at("d", h, p.zz), spot, spot, to_z(p.out), p.out_d)
-        start(at_core(h, "d", p.zz), spot, spot, to_core)
+        start(at_core(h, "d"), spot, spot, to_core)
 
     loaded = []
 
     def product(h, column):
-        for zz in range(n_z):
-            arrived(at_core(h, column, zz), held.at[block(column, 1 - core, zz, h)])
+        arrived(at_core(h, column), held.at[pl.ds(block(column, 1 - core, 0, h), n_z)])
         if not loaded:
             for load in loads:
                 load.wait()
@@ -492,8 +493,8 @@
             )
         if i == 0 or p.maybe_far:
             condition = p.far if i else None
-            start(at("dx", h, p.zz), part.at[spot, pl.ds(half, half)], x_diag.at[h * n_z + p.zz], to_x, condition)
-            start(at("dy", h, p.zz), part.at[spot, pl.ds(0, half)], y_diag.at[h * n_z + p.zz], to_y, condition)
+            start(at_far("dx", h, i), part.at[spot, pl.ds(half, half)], x_diag.at[h * n_z + p.zz], to_x, condition)
+            start(at_far("dy", h, i), part.at[spot, pl.ds(0, half)], y_diag.at[h * n_z + p.zz], to_y, condition)
 
     def give_x(h, i):
         p = planes[i]
@@ -501,11 +502,11 @@
         index = h * n_z + p.zz
         spot = combined(h, "x", p.zz)
         if i == 0 or p.maybe_far:
-            arrived(at("dy", h, p.zz), y_diag.at[index], p.far if i else None)
+            arrived(at_far("dy", h, i), y_diag.at[index], p.far if i else None)
             part[spot, :half] = (
                 part[spot, :half].astype(jnp.float32) + y_diag[index].astype(jnp.float32)
             ).astype(part.dtype)
-        start(at("rx", h, p.zz), part.at[spot], x_in.at[index], to_x)
+        start(at("sides", h, p.zz), part.at[spot], sides_in.at[2 * index], to_x)
 
     def give_y(h, i):
         p = planes[i]
@@ -513,11 +514,11 @@
         index = h * n_z + p.zz
         spot = combined(h, "y", p.zz)
         if i == 0 or p.maybe_far:
-            arrived(at("dx", h, p.zz), x_diag.at[index], p.far if i else None)
+            arrived(at_far("dx", h, i), x_diag.at[index], p.far if i else None)
             part[spot, half:] = (
                 part[spot, half:].astype(jnp.float32) + x_diag[index].astype(jnp.float32)
             ).astype(part.dtype)
-        start(at("ry", h, p.zz), part.at[spot], y_in.at[index], to_y)
+        start(at("sides", h, p.zz), part.at[spot], sides_in.at[2 * index + 1], to_y)
 
     def give_xy(h, i):
         give_x(h, i)
@@ -528,18 +529,17 @@
         base = h * (n_z + 1)
         index = h * n_z + p.zz
         need(h, "o")
-        arrived(at("rx", h, p.zz), x_in.at[index])
-        arrived(at("ry", h, p.zz), y_in.at[index])
+        arrived(at("sides", h, p.zz), sides_in.at[pl.ds(2 * index, 2)])
         if i == 0:
             arrived(at_chain("oc", h, z), o_chain.at[base + z], below)
             arrived(at_chain("oc", h, n_z), o_chain.at[base + n_z], above)
             combined(
-                h, "o", z, (x_in, index), (y_in, index), (o_chain, base + z), (o_chain, base + n_z),
+                h, "o", z, (sides_in, 2 * index), (sides_in, 2 * index + 1), (o_chain, base + z), (o_chain, base + n_z),
                 target=h * rows,
             )
         else:
             arrived(at_chain("oc", h, p.zz), o_chain.at[base + p.zz], p.has_out)
-            spot = combined(h, "o", p.zz, (x_in, index), (y_in, index), (o_chain, base + p.zz))
+            spot = combined(h, "o", p.zz, (sides_in, 2 * index), (sides_in, 2 * index + 1), (o_chain, base + p.zz))
             start(at_chain("oc", h, slot_at(p)), part.at[spot], o_chain.at[base + slot_at(p)], to_z(p.back))
 
     steps = {
@@ -548,15 +548,15 @@
     }
     for name, *numbers in PLAN:
         steps[name](*numbers)
-    for condition, copy in sent:
+    for condition, copy in sent[-SENDS:]:
         when(condition, copy.wait_send)
 
 
-RECV = {kind: (lambda n_z, batches: n_z * batches) for kind in ("x", "y", "o", "d", "x2", "y2", "dx", "dy", "rx", "ry")}
-RECV["core"] = lambda n_z, batches: 4 * n_z * batches
-RECV["p"] = lambda n_z, batches: 4 * batches
+RECV = {kind: (lambda n_z, batches: n_z * batches) for kind in ("x", "y", "o", "d", "sides")}
+RECV["halves"] = RECV["dx"] = RECV["dy"] = lambda n_z, batches: (n_z - n_z // 2) * batches
+RECV["core"] = RECV["p"] = lambda n_z, batches: 4 * batches
 RECV["dc"] = RECV["oc"] = lambda n_z, batches: (n_z + 1) * batches
-
+SENDS = 48
 
 BATCHES = 2
 
@@ -647,7 +647,6 @@
     lanes = round_up(width + 2 * n_exp, LANES)
     total = n_exp * lax.axis_size("dp") * batches
     receives = sum(size(n_z, batches) for size in RECV.values())
-    sends = 64 * n_z
     bf16 = jnp.bfloat16
     in_vmem = pl.BlockSpec(memory_space=pltpu.VMEM)
     anywhere = pl.BlockSpec(memory_space=pl.ANY)
@@ -663,8 +662,7 @@
             pltpu.VMEM((total, rows, lanes), bf16),
             pltpu.VMEM((total, rows, width), bf16),
             pltpu.VMEM((total // 2, rows, width), bf16),
-            pltpu.VMEM((batches * n_z, rows, width), bf16),
-            pltpu.VMEM((batches * n_z, rows, width), bf16),
+            pltpu.VMEM((batches * n_z * 2, rows, width), bf16),
             pltpu.VMEM((batches * n_z, rows // 2, width), bf16),
             pltpu.VMEM((batches * n_z, rows // 2, width), bf16),
             pltpu.VMEM((batches * (n_z + 1), rows, width), bf16),
@@ -672,7 +670,7 @@
             pltpu.VMEM((width, hidden_width), bf16),
             pltpu.VMEM((width, hidden_width), bf16),
             pltpu.VMEM((width, hidden_width), bf16),
-            pltpu.SemaphoreType.DMA((sends,)),
+            pltpu.SemaphoreType.DMA((SENDS,)),
             pltpu.SemaphoreType.DMA((receives,)),
             pltpu.SemaphoreType.DMA((6,)),
         ],

time: 96.5 us -> 94.1 us (0.975)
  Pallas kernels: 95.5 us -> 93.2 us
    pallas_call x1, Pallas kernels: 95.5 us -> 93.2 us  [fused_device(): pl.pallas_call(functools.partial(fused_kernel, n_exp), in_specs=[anywhere...]
where the time goes in v3:
time: 94.1 us; the launch traced here: 93.9 us
  Pallas kernels  93.2 us (99%)
    pallas_call x1, Pallas kernels, fused_device(): pl.pallas_call(functools.partial(fused_kernel, n_exp), in_specs=[anywhere...  93.2 us

profile of v3, /device:TPU:0, one launch (start us, length us, event | category | flops | bytes accessed | tf_op | source)
XLA Modules:
  0.0 93.9 jit_solution(2300119701935797781)
XLA Ops:
  0.0 93.2 %shard_map.64 = bf16[64,2880]{1,0:T(8,128)(2,1)S(1)} custom-call(bf16[64,2880]{1,0:T(8,128)(2,1)} %tok_hbm.1, s32[4,64]{1,0:T(4,128)} %bitcast.10, f32[4,64]{1,0:T(4,128)} %bitcast.11, bf16[2880,384]{1,0:T(8,128)(2,1)} %bitcast.7, bf16[2880,384]{1,0:T(8,128)(2,1)} %bitcast.8, bf16[2880,384]{1,0:T(8,128)(2,1)} %bitcast.9), custom_call_target="tpu_custom_call" | custom-call | tf_op jit(solution)/shard_map/pallas_call | solution.py:653
  93.2 0.7 copy.8

commit v4 on v3

--- a/solution.py
+++ b/solution.py
@@ -556,7 +556,7 @@
 RECV["halves"] = RECV["dx"] = RECV["dy"] = lambda n_z, batches: (n_z - n_z // 2) * batches
 RECV["core"] = RECV["p"] = lambda n_z, batches: 4 * batches
 RECV["dc"] = RECV["oc"] = lambda n_z, batches: (n_z + 1) * batches
-SENDS = 48
+SENDS = 40
 
 BATCHES = 2
 

time: 94.1 us -> 94 us (level)
  no operation moved by 1% of the time
where the time goes in v4:
time: 94 us; the launch traced here: 93.8 us
  Pallas kernels  93 us (99%)
    pallas_call x1, Pallas kernels, fused_device(): pl.pallas_call(functools.partial(fused_kernel, n_exp), in_specs=[anywhere...  93 us

profile of v4, /device:TPU:0, one launch (start us, length us, event | category | flops | bytes accessed | tf_op | source)
XLA Modules:
  0.0 93.8 jit_solution(14586904845866574948)
XLA Ops:
  0.0 93.0 %shard_map.64 = bf16[64,2880]{1,0:T(8,128)(2,1)S(1)} custom-call(bf16[64,2880]{1,0:T(8,128)(2,1)} %tok_hbm.1, s32[4,64]{1,0:T(4,128)} %bitcast.10, f32[4,64]{1,0:T(4,128)} %bitcast.11, bf16[2880,384]{1,0:T(8,128)(2,1)} %bitcast.7, bf16[2880,384]{1,0:T(8,128)(2,1)} %bitcast.8, bf16[2880,384]{1,0:T(8,128)(2,1)} %bitcast.9), custom_call_target="tpu_custom_call" | custom-call | tf_op jit(solution)/shard_map/pallas_call | solution.py:653
  93.0 0.7 copy.8
